TPU v7x, 32 devices: a whole 2x2x4 slice. The times are simulated.
32 devices in a mesh: dp: 8 (over z, y), tensor: 4 (over x, core).
Axes of the slice: x: 2, y: 2, z: 4, core: 2. Of those that a mesh axis runs over, the one named last changes fastest.
Arguments:
- layer_input: bfloat16 [3072, 2304], P('dp'), may hold values from -6 to 6
- cotangent: bfloat16 [3072, 2304], P('dp'), may hold values from -6 to 6
- seq_lengths: int32 [8, 8], P('dp'), may hold values from 0 to 256, as said below
- norm_attn_in: float32 [2304], replicated, may hold values from 0.1 to 1.9
- w_query: bfloat16 [2304, 2048], P('dp', 'tensor'), may hold values from -1 to 1
- w_key: bfloat16 [2304, 1024], P('dp', 'tensor'), may hold values from -1 to 1
- w_value: bfloat16 [2304, 1024], P('dp', 'tensor'), may hold values from -0.125 to 0.125
- w_out: bfloat16 [2048, 2304], P('tensor', 'dp'), may hold values from -0.125 to 0.125
- norm_attn_out: float32 [2304], replicated, may hold values from 0.1 to 1.9
- norm_ffn_in: float32 [2304], replicated, may hold values from 0.1 to 1.9
- w_gate: bfloat16 [2304, 9216], P('dp', 'tensor'), may hold values from -0.125 to 0.125
- w_up: bfloat16 [2304, 9216], P('dp', 'tensor'), may hold values from -0.125 to 0.125
- w_down: bfloat16 [9216, 2304], P('tensor', 'dp'), may hold values from -0.0625 to 0.0625
- norm_ffn_out: float32 [2304], replicated, may hold values from 0.1 to 1.9
Outputs:
- layer_output: bfloat16 [3072, 2304], P('dp')
- input_grad: float32 [3072, 2304], P('dp')
- grad_norm_attn_in: float32 [2304], P('dp')
- grad_w_query: float32 [2304, 2048], P('dp', 'tensor')
- grad_w_key: float32 [2304, 1024], P('dp', 'tensor')
- grad_w_value: float32 [2304, 1024], P('dp', 'tensor')
- grad_w_out: float32 [2048, 2304], P('tensor', 'dp')
- grad_norm_attn_out: float32 [2304], P('dp')
- grad_norm_ffn_in: float32 [2304], P('dp')
- grad_w_gate: float32 [2304, 9216], P('dp', 'tensor')
- grad_w_up: float32 [2304, 9216], P('dp', 'tensor')
- grad_w_down: float32 [9216, 2304], P('tensor', 'dp')
- grad_norm_ffn_out: float32 [2304], P('dp')
Inputs may be any that keep to these rules, and one draw needn't show every extreme that they name: `seq_lengths`: row r lists the lengths of the sequences on data index r in packing order; slots after the last sequence hold 0. Each row sums to at most 384 and some row sums to exactly 384; some sequence has exactly 256 tokens.
All inputs are finite; a program needn't handle non-finite values.
Results may differ from a plain program's by a relative error of at most 0.02.
The roundings to bfloat16 on the way count: a program that leaves them out, or rounds other values in their place, can miss the bound.
Values may be sent and summed in bfloat16 or wider, within the bound.
A program may use at most 256 MiB of HBM per device.

v0:
```python
import math
import jax
import jax.numpy as jnp
from jax import lax
from jax.sharding import PartitionSpec as P

H = 8
KV = 4
HD = 256
EPSILON = 1e-06
SOFT_CAP = 50.0
QUERY_SCALE = 0.0625
GELU_COEFF = 0.7978845608028654


def rms_scale(values, scales):
    return values * lax.rsqrt(jnp.mean(values * values, axis=-1, keepdims=True) + EPSILON) * scales


def gelu_tanh(inputs):
    return (
        0.5 * inputs * (1.0 + jnp.tanh(GELU_COEFF * (inputs + 0.044715 * inputs * inputs * inputs)))
    )


def rotate_half(heads):
    middle = heads.shape[-1] // 2
    return jnp.concatenate([-heads[..., middle:], heads[..., :middle]], axis=-1)


def layout(lengths, row_count):
    seq_ends = jnp.cumsum(lengths)
    row_index = jnp.arange(row_count, dtype=jnp.int32)
    passed = (row_index[:, None] >= seq_ends[None, :]).astype(jnp.int32)
    segment = jnp.sum(passed, axis=1)
    is_live = row_index < seq_ends[-1]
    seq_ident = jnp.where(is_live, segment, lengths.shape[0] + row_index)
    offset = row_index - jnp.sum(passed * lengths[None, :], axis=1)
    allowed = (seq_ident[:, None] == seq_ident[None, :]) & (
        row_index[None, :] <= row_index[:, None]
    )
    middle = HD // 2
    inverse = jnp.exp(jnp.arange(middle, dtype=jnp.float32) * (-2.0 * math.log(10000.0) / HD))
    angles = offset.astype(jnp.float32)[:, None] * inverse[None, :]
    cosine = jnp.concatenate([jnp.cos(angles), jnp.cos(angles)], axis=1)
    sine_wave = jnp.concatenate([jnp.sin(angles), jnp.sin(angles)], axis=1)
    return (is_live, allowed, cosine, sine_wave)


def matmul(left, right):
    return jnp.dot(left, right, preferred_element_type=jnp.float32)


def left_product(left, right):
    return jnp.einsum("td,tc->dc", left, right, preferred_element_type=jnp.float32)


def right_product(left, right):
    return jnp.einsum("tc,dc->td", left, right, preferred_element_type=jnp.float32)


def capped_scores(query, keys):
    raw_scores = jnp.einsum("kgqd,ksd->kgqs", query, keys, preferred_element_type=jnp.float32)
    return SOFT_CAP * jnp.tanh(raw_scores / SOFT_CAP)


def shards(
    layer_input,
    cotangent,
    seq_lengths,
    norm_attn_in,
    w_query,
    w_key,
    w_value,
    w_out,
    norm_attn_out,
    norm_ffn_in,
    w_gate,
    w_up,
    w_down,
    norm_ffn_out,
):
    gathered = (
        lax.all_gather(w_query, "dp", axis=0, tiled=True),
        lax.all_gather(w_key, "dp", axis=0, tiled=True),
        lax.all_gather(w_value, "dp", axis=0, tiled=True),
        lax.all_gather(w_out, "dp", axis=1, tiled=True),
        lax.all_gather(w_gate, "dp", axis=0, tiled=True),
        lax.all_gather(w_up, "dp", axis=0, tiled=True),
        lax.all_gather(w_down, "dp", axis=1, tiled=True),
    )
    query_full, key_full, value_full, out_full, gate_full, up_full, down_full = gathered
    row_count = layer_input.shape[0]
    is_live, allowed, cosine, sine_wave = layout(seq_lengths[0], row_count)
    kv_heads = key_full.shape[1] // HD
    groups = H // KV
    layer_float = layer_input.astype(jnp.float32)
    h_attn = rms_scale(layer_float, norm_attn_in).astype(jnp.bfloat16)
    query_pre = (
        matmul(h_attn, query_full).reshape(row_count, kv_heads, groups, HD).transpose(1, 2, 0, 3)
    )
    query = ((query_pre * cosine + rotate_half(query_pre) * sine_wave) * QUERY_SCALE).astype(
        jnp.bfloat16
    )
    key_pre = matmul(h_attn, key_full).reshape(row_count, kv_heads, HD).transpose(1, 0, 2)
    keys = (key_pre * cosine + rotate_half(key_pre) * sine_wave).astype(jnp.bfloat16)
    values = (
        matmul(h_attn, value_full)
        .astype(jnp.bfloat16)
        .reshape(row_count, kv_heads, HD)
        .transpose(1, 0, 2)
    )
    capped = capped_scores(query, keys)
    expo = jnp.where(allowed, jnp.exp(capped), 0.0)
    log_total = jnp.log(jnp.sum(expo, axis=-1, keepdims=True))
    probs = jnp.where(allowed, jnp.exp(capped - log_total), 0.0).astype(jnp.bfloat16)
    mixed = jnp.einsum("kgqs,ksd->kgqd", probs, values, preferred_element_type=jnp.float32).astype(
        jnp.bfloat16
    )
    mixed_flat = mixed.transpose(2, 0, 1, 3).reshape(row_count, -1)
    attn_branch = lax.psum(matmul(mixed_flat, out_full), "tensor")
    resid = layer_float + rms_scale(attn_branch, norm_attn_out)
    h_ffn = rms_scale(resid, norm_ffn_in).astype(jnp.bfloat16)
    gate_pre = matmul(h_ffn, gate_full)
    up_pre = matmul(h_ffn, up_full)
    gelu_gate = gelu_tanh(gate_pre)
    hidden = (gelu_gate * up_pre).astype(jnp.bfloat16)
    ffn_branch = lax.psum(matmul(hidden, down_full), "tensor")
    layer_output = (resid + rms_scale(ffn_branch, norm_ffn_out)).astype(jnp.bfloat16)
    query_back, key_back, value_back, out_back, gate_back, up_back, down_back = gathered
    grad_out = cotangent.astype(jnp.float32) * is_live[:, None].astype(jnp.float32)
    _, pull_four = jax.vjp(rms_scale, ffn_branch, norm_ffn_out)
    grad_ffn_float, grad_norm_ffn_out = pull_four(grad_out)
    grad_ffn_branch = grad_ffn_float.astype(jnp.bfloat16)
    grad_w_down = left_product(hidden, grad_ffn_branch)
    grad_hidden = right_product(grad_ffn_branch, down_back)
    grad_up = (grad_hidden * gelu_gate).astype(jnp.bfloat16)
    _, pull_gelu = jax.vjp(gelu_tanh, gate_pre)
    grad_gate = pull_gelu(grad_hidden * up_pre)[0].astype(jnp.bfloat16)
    grad_w_gate = left_product(h_ffn, grad_gate)
    grad_w_up = left_product(h_ffn, grad_up)
    grad_h_ffn = lax.psum(
        right_product(grad_gate, gate_back) + right_product(grad_up, up_back), "tensor"
    )
    _, pull_three = jax.vjp(rms_scale, resid, norm_ffn_in)
    grad_resid_part, grad_norm_ffn_in = pull_three(grad_h_ffn)
    grad_resid = grad_out + grad_resid_part
    _, pull_two = jax.vjp(rms_scale, attn_branch, norm_attn_out)
    grad_attn_float, grad_norm_attn_out = pull_two(grad_resid)
    grad_attn_branch = grad_attn_float.astype(jnp.bfloat16)
    grad_w_out = left_product(mixed_flat, grad_attn_branch)
    grad_mixed = right_product(grad_attn_branch, out_back).astype(jnp.bfloat16)
    grad_mixed = grad_mixed.reshape(row_count, kv_heads, groups, HD).transpose(1, 2, 0, 3)
    capped_back = capped_scores(query, keys)
    weights_back = jnp.where(allowed, jnp.exp(capped_back - log_total), 0.0)
    grad_values = jnp.einsum(
        "kgqs,kgqd->ksd",
        weights_back.astype(jnp.bfloat16),
        grad_mixed,
        preferred_element_type=jnp.float32,
    ).astype(jnp.bfloat16)
    grad_probs = jnp.einsum(
        "kgqd,ksd->kgqs", grad_mixed, values, preferred_element_type=jnp.float32
    )
    row_delta = jnp.sum(weights_back * grad_probs, axis=-1, keepdims=True)
    tanh_part = capped_back / SOFT_CAP
    grad_scores = (weights_back * (grad_probs - row_delta) * (1.0 - tanh_part * tanh_part)).astype(
        jnp.bfloat16
    )
    grad_query_raw = jnp.einsum(
        "kgqs,ksd->kgqd", grad_scores, keys, preferred_element_type=jnp.float32
    )
    grad_query = (
        (grad_query_raw * cosine - rotate_half(grad_query_raw) * sine_wave) * QUERY_SCALE
    ).astype(jnp.bfloat16)
    grad_keys_raw = jnp.einsum(
        "kgqs,kgqd->ksd", grad_scores, query, preferred_element_type=jnp.float32
    )
    grad_keys = (grad_keys_raw * cosine - rotate_half(grad_keys_raw) * sine_wave).astype(
        jnp.bfloat16
    )
    grad_query_flat = grad_query.transpose(2, 0, 1, 3).reshape(row_count, -1)
    grad_keys_flat = grad_keys.transpose(1, 0, 2).reshape(row_count, -1)
    grad_values_flat = grad_values.transpose(1, 0, 2).reshape(row_count, -1)
    grad_w_query = left_product(h_attn, grad_query_flat)
    grad_w_key = left_product(h_attn, grad_keys_flat)
    grad_w_value = left_product(h_attn, grad_values_flat)
    local_h_attn = (
        right_product(grad_query_flat, query_back)
        + right_product(grad_keys_flat, key_back)
        + right_product(grad_values_flat, value_back)
    )
    grad_h_attn = lax.psum(local_h_attn.astype(jnp.bfloat16), "tensor").astype(jnp.float32)
    _, pull_one = jax.vjp(rms_scale, layer_float, norm_attn_in)
    grad_input_part, grad_norm_attn_in = pull_one(grad_h_attn)
    input_grad = grad_resid + grad_input_part
    summed = (
        lax.psum_scatter(
            grad_norm_attn_in.astype(jnp.bfloat16), "dp", scatter_dimension=0, tiled=True
        ).astype(jnp.float32),
        lax.psum_scatter(
            grad_w_query.astype(jnp.bfloat16), "dp", scatter_dimension=0, tiled=True
        ).astype(jnp.float32),
        lax.psum_scatter(
            grad_w_key.astype(jnp.bfloat16), "dp", scatter_dimension=0, tiled=True
        ).astype(jnp.float32),
        lax.psum_scatter(
            grad_w_value.astype(jnp.bfloat16), "dp", scatter_dimension=0, tiled=True
        ).astype(jnp.float32),
        lax.psum_scatter(
            grad_w_out.astype(jnp.bfloat16), "dp", scatter_dimension=1, tiled=True
        ).astype(jnp.float32),
        lax.psum_scatter(
            grad_norm_attn_out.astype(jnp.bfloat16), "dp", scatter_dimension=0, tiled=True
        ).astype(jnp.float32),
        lax.psum_scatter(
            grad_norm_ffn_in.astype(jnp.bfloat16), "dp", scatter_dimension=0, tiled=True
        ).astype(jnp.float32),
        lax.psum_scatter(
            grad_w_gate.astype(jnp.bfloat16), "dp", scatter_dimension=0, tiled=True
        ).astype(jnp.float32),
        lax.psum_scatter(
            grad_w_up.astype(jnp.bfloat16), "dp", scatter_dimension=0, tiled=True
        ).astype(jnp.float32),
        lax.psum_scatter(
            grad_w_down.astype(jnp.bfloat16), "dp", scatter_dimension=1, tiled=True
        ).astype(jnp.float32),
        lax.psum_scatter(
            grad_norm_ffn_out.astype(jnp.bfloat16), "dp", scatter_dimension=0, tiled=True
        ).astype(jnp.float32),
    )
    (
        sum_attn_in,
        sum_query,
        sum_key,
        sum_value,
        sum_out,
        sum_attn_out,
        sum_ffn_in,
        sum_gate,
        sum_up,
        sum_down,
        sum_ffn_out,
    ) = summed
    return (
        layer_output,
        input_grad,
        sum_attn_in,
        sum_query,
        sum_key,
        sum_value,
        sum_out,
        sum_attn_out,
        sum_ffn_in,
        sum_gate,
        sum_up,
        sum_down,
        sum_ffn_out,
    )


def solution(mesh):
    placed = (
        P("dp", None),
        P("dp", None),
        P("dp", None),
        P(),
        P("dp", "tensor"),
        P("dp", "tensor"),
        P("dp", "tensor"),
        P("tensor", "dp"),
        P(),
        P(),
        P("dp", "tensor"),
        P("dp", "tensor"),
        P("tensor", "dp"),
        P(),
    )
    return jax.shard_map(
        shards,
        mesh=mesh,
        in_specs=placed,
        out_specs=(
            P("dp", None),
            P("dp", None),
            P("dp"),
            P("dp", "tensor"),
            P("dp", "tensor"),
            P("dp", "tensor"),
            P("tensor", "dp"),
            P("dp"),
            P("dp"),
            P("dp", "tensor"),
            P("dp", "tensor"),
            P("tensor", "dp"),
            P("dp"),
        ),
        check_vma=False,
    )
```

profile of v0, /device:TPU:0, one launch (start us, length us, event | category | flops | bytes accessed | tf_op | source)
XLA Modules:
  0.0 1854.5 jit_solution(15311761673181839978)
XLA Ops:
  15.7 38.3 %all-gather.10.cloned.1.call-done = bf16[2304,256]{1,0:T(8,128)(2,1)} async-done(((bf16[288,256]{1,0:T(8,128)(2,1)}), bf16[2304,256]{1,0:T(8,128)(2,1)}) %all-gather.10.cloned.1.call-update) | async-done | bytes 1179664 | tf_op jit(solution)/shard_map/all_gather | solution.py:85
  57.0 39.1 %all-gather.12.cloned.1.call-done = bf16[2304,256]{1,0:T(8,128)(2,1)} async-done(((bf16[288,256]{1,0:T(8,128)(2,1)}), bf16[2304,256]{1,0:T(8,128)(2,1)}) %all-gather.12.cloned.1.call-update) | async-done | bytes 1179664 | tf_op jit(solution)/shard_map/all_gather | solution.py:86
  98.0 50.8 %all-gather.8.cloned.1.call-done = bf16[2304,512]{1,0:T(8,128)(2,1)} async-done(((bf16[288,512]{1,0:T(8,128)(2,1)}), bf16[2304,512]{1,0:T(8,128)(2,1)}) %all-gather.8.cloned.1.call-update) | async-done | bytes 2359312 | tf_op jit(solution)/shard_map/all_gather | solution.py:84
  154.2 47.0 %all-gather.14.cloned.1.call-done = bf16[512,2304]{0,1:T(8,128)(2,1)} async-done(((bf16[512,288]{0,1:T(8,128)(2,1)}), bf16[512,2304]{0,1:T(8,128)(2,1)}) %all-gather.14.cloned.1.call-update) | async-done | bytes 2359312 | tf_op jit(solution)/shard_map/all_gather | solution.py:87
  208.1 71.2 %all-reduce.10.cloned.1.call-done = f32[384,2304]{1,0:T(8,128)} async-done(((f32[384,2304]{1,0:T(8,128)}), f32[384,2304]{1,0:T(8,128)}) %all-reduce.10.cloned.1.call-update) | async-done | bytes 3538960 | tf_op jit(solution)/shard_map/psum | solution.py:121
  287.5 146.2 %all-gather.16.cloned.1.call-done = bf16[2304,2304]{1,0:T(8,128)(2,1)} async-done(((bf16[288,2304]{1,0:T(8,128)(2,1)}), bf16[2304,2304]{1,0:T(8,128)(2,1)}) %all-gather.16.cloned.1.call-update) | async-done | bytes 10616848 | tf_op jit(solution)/shard_map/all_gather | solution.py:88
  433.7 10.6 fusion.100
  444.3 141.9 %all-gather.18.cloned.1.call-done = bf16[2304,2304]{1,0:T(8,128)(2,1)} async-done(((bf16[288,2304]{1,0:T(8,128)(2,1)}), bf16[2304,2304]{1,0:T(8,128)(2,1)}) %all-gather.18.cloned.1.call-update) | async-done | bytes 10616848 | tf_op jit(solution)/shard_map/all_gather | solution.py:89
  586.2 12.3 multiply_convert_fusion.1
  598.5 140.2 %all-gather.20.cloned.1.call-done = bf16[2304,2304]{0,1:T(8,128)(2,1)} async-done(((bf16[2304,288]{0,1:T(8,128)(2,1)}), bf16[2304,2304]{0,1:T(8,128)(2,1)}) %all-gather.20.cloned.1.call-update) | async-done | bytes 10616848 | tf_op jit(solution)/shard_map/all_gather | solution.py:90
  738.7 10.6 fusion.101
  750.8 71.7 %all-reduce.12.cloned.1.call-done = f32[384,2304]{1,0:T(8,128)} async-done(((f32[384,2304]{1,0:T(8,128)}), f32[384,2304]{1,0:T(8,128)}) %all-reduce.12.cloned.1.call-update) | async-done | bytes 3538960 | tf_op jit(solution)/shard_map/psum | solution.py:128
  830.6 13.1 multiply_convert_fusion
  851.5 12.9 convolution_add_fusion.2
  868.4 71.1 %all-reduce.14.cloned.1.call-done = f32[384,2304]{1,0:T(8,128)} async-done(((f32[384,2304]{1,0:T(8,128)}), f32[384,2304]{1,0:T(8,128)}) %all-reduce.14.cloned.1.call-update) | async-done | bytes 3538960 | tf_op jit(solution)/shard_map/psum | solution.py:142
  1003.0 10.7 convolution_convert_fusion
  1019.7 38.6 %all-reduce.4 = (bf16[2304]{0:T(1024)(128)(2,1)}, bf16[2304]{0:T(1024)(128)(2,1)}, bf16[2304]{0:T(1024)(128)(2,1)}, bf16[2304]{0:T(1024)(128)(2,1)}) all-reduce(bf16[2304]{0:T(1024)(128)(2,1)} %get-tuple-element.19, bf16[2304]{0:T(1024)(128)(2,1)} %get-tuple-element.15, ...), channel_id=2, replica_groups=mesh['dp'=8,'tensor'=4] {'dp'}, use_global_device_ids=true, to_apply=%region_18.19.clone | all-reduce | flops 9216 | bytes 36864
  1066.6 17.3 reduce-scatter.10.cloned.1.call-done
  1085.5 65.6 %reduce-scatter.12.cloned.1.call-done = bf16[288,256]{1,0:T(8,128)(2,1)} async-done(((bf16[2304,256]{1,0:T(8,128)(2,1)}), bf16[288,256]{1,0:T(8,128)(2,1)}) %reduce-scatter.12.cloned.1.call-update) | async-done | bytes 147472 | tf_op jit(solution)/shard_map/reduce_scatter | solution.py:207
  1152.7 70.9 %reduce-scatter.8.cloned.1.call-done = bf16[288,512]{1,0:T(8,128)(2,1)} async-done(((bf16[2304,512]{1,0:T(8,128)(2,1)}), bf16[288,512]{1,0:T(8,128)(2,1)}) %reduce-scatter.8.cloned.1.call-update) | async-done | bytes 294928 | tf_op jit(solution)/shard_map/reduce_scatter | solution.py:201
  1225.5 70.9 %reduce-scatter.14.cloned.1.call-done = bf16[512,288]{0,1:T(8,128)(2,1)} async-done(((bf16[512,2304]{0,1:T(8,128)(2,1)}), bf16[512,288]{0,1:T(8,128)(2,1)}) %reduce-scatter.14.cloned.1.call-update) | async-done | bytes 294928 | tf_op jit(solution)/shard_map/reduce_scatter | solution.py:210
  1298.2 180.9 %reduce-scatter.16.cloned.1.call-done = bf16[288,2304]{1,0:T(8,128)(2,1)} async-done(((bf16[2304,2304]{1,0:T(8,128)(2,1)}), bf16[288,2304]{1,0:T(8,128)(2,1)}) %reduce-scatter.16.cloned.1.call-update) | async-done | bytes 1327120 | tf_op jit(solution)/shard_map/reduce_scatter | solution.py:219
  1482.2 179.6 %reduce-scatter.18.cloned.1.call-done = bf16[288,2304]{1,0:T(8,128)(2,1)} async-done(((bf16[2304,2304]{1,0:T(8,128)(2,1)}), bf16[288,2304]{1,0:T(8,128)(2,1)}) %reduce-scatter.18.cloned.1.call-update) | async-done | bytes 1327120 | tf_op jit(solution)/shard_map/reduce_scatter | solution.py:222
  1664.8 179.7 %reduce-scatter.20.cloned.1.call-done = bf16[2304,288]{0,1:T(8,128)(2,1)} async-done(((bf16[2304,2304]{0,1:T(8,128)(2,1)}), bf16[2304,288]{0,1:T(8,128)(2,1)}) %reduce-scatter.20.cloned.1.call-update) | async-done | bytes 1327120 | tf_op jit(solution)/shard_map/reduce_scatter | solution.py:225
  (229 shorter events, 147.4 us)
Async XLA Ops:
  7.2 46.9 %all-gather.10.cloned.1.call-start = ((), (), s32[]{:S(2)}) async-start(), calls=%async_computation.8 | async-start | bytes 1327104 | tf_op jit(solution)/shard_map/all_gather | solution.py:85
  7.9 88.2 %all-gather.12.cloned.1.call-start = ((), (), s32[]{:S(2)}) async-start(), calls=%async_computation.9 | async-start | bytes 1327104 | tf_op jit(solution)/shard_map/all_gather | solution.py:86
  8.7 140.1 %all-gather.8.cloned.1.call-start = ((), (), s32[]{:S(2)}) async-start(), calls=%async_computation.7 | async-start | bytes 2654208 | tf_op jit(solution)/shard_map/all_gather | solution.py:84
  9.4 191.8 %all-gather.14.cloned.1.call-start = ((), (), s32[]{:S(2)}) async-start(), calls=%async_computation.10 | async-start | bytes 2654208 | tf_op jit(solution)/shard_map/all_gather | solution.py:87
  10.0 269.4 %all-reduce.10.cloned.1.call-start = ((), (), s32[]{:S(2)}) async-start(), calls=%async_computation.11 | async-start | bytes 7077888 | tf_op jit(solution)/shard_map/psum | solution.py:121
  14.1 134.7 %copy-start.50 = (f32[384]{0:T(512)}, f32[384]{0:T(512)S(1)}, u32[]{:S(2)}) copy-start(f32[384]{0:T(512)S(1)} %fusion.69) | copy-start | bytes 4612
  14.9 138.5 %copy-start.33 = (pred[384,384]{0,1:T(8,128)(4,1)}, pred[384,384]{0,1:T(8,128)(4,1)S(1)}, u32[]{:S(2)}) copy-start(pred[384,384]{0,1:T(8,128)(4,1)S(1)} %fusion.50) | copy-start | bytes 442372
  15.7 80.3 %copy-start.4 = (bf16[384,2304]{1,0:T(8,128)(2,1)S(1)}, bf16[384,2304]{1,0:T(8,128)(2,1)}, u32[]{:S(2)}) copy-start(bf16[384,2304]{1,0:T(8,128)(2,1)} %param.14) | copy-start | bytes 5308420
  56.9 95.1 %copy-start.10 = (f32[384,256]{0,1:T(8,128)}, f32[384,256]{0,1:T(8,128)S(1)}, u32[]{:S(2)}) copy-start(f32[384,256]{0,1:T(8,128)S(1)} %get-tuple-element.42) | copy-start | bytes 1179652
  57.0 95.1 %copy-start.12 = (f32[384,256]{0,1:T(8,128)}, f32[384,256]{0,1:T(8,128)S(1)}, u32[]{:S(2)}) copy-start(f32[384,256]{0,1:T(8,128)S(1)} %get-tuple-element.43) | copy-start | bytes 1179652
  57.0 95.3 %copy-start.27 = (bf16[384,256,1]{0,1,2:T(8,128)(2,1)}, bf16[384,256,1]{0,1,2:T(8,128)(2,1)S(1)}, u32[]{:S(2)}) copy-start(bf16[384,256,1]{0,1,2:T(8,128)(2,1)S(1)} %get-tuple-element.41) | copy-start | bytes 589828
  205.8 227.8 %all-gather.16.cloned.1.call-start = ((), (), s32[]{:S(2)}) async-start(), calls=%async_computation.12 | async-start | bytes 11943936 | tf_op jit(solution)/shard_map/all_gather | solution.py:88
  206.4 379.8 %all-gather.18.cloned.1.call-start = ((), (), s32[]{:S(2)}) async-start(), calls=%async_computation.13 | async-start | bytes 11943936 | tf_op jit(solution)/shard_map/all_gather | solution.py:89
  207.2 531.5 %all-gather.20.cloned.1.call-start = ((), (), s32[]{:S(2)}) async-start(), calls=%async_computation.14 | async-start | bytes 11943936 | tf_op jit(solution)/shard_map/all_gather | solution.py:90
  207.9 614.6 %all-reduce.12.cloned.1.call-start = ((), (), s32[]{:S(2)}) async-start(), calls=%async_computation.15 | async-start | bytes 7077888 | tf_op jit(solution)/shard_map/psum | solution.py:128
  749.3 190.2 %all-reduce.14.cloned.1.call-start = ((), (), s32[]{:S(2)}) async-start(), calls=%async_computation.16 | async-start | bytes 7077888 | tf_op jit(solution)/shard_map/psum | solution.py:142
  864.5 151.3 %all-reduce.16.cloned.1.call-start = ((), (), s32[]{:S(2)}) async-start(), calls=%async_computation.17 | async-start | bytes 3538944 | tf_op jit(solution)/shard_map/psum | solution.py:193
  969.3 114.5 %reduce-scatter.10.cloned.1.call-start = ((), (), s32[]{:S(2)}) async-start(), calls=%async_computation.19 | async-start | bytes 1327104 | tf_op jit(solution)/shard_map/reduce_scatter | solution.py:204
  971.4 179.7 %reduce-scatter.12.cloned.1.call-start = ((), (), s32[]{:S(2)}) async-start(), calls=%async_computation.20 | async-start | bytes 1327104 | tf_op jit(solution)/shard_map/reduce_scatter | solution.py:207
  973.5 250.2 %reduce-scatter.8.cloned.1.call-start = ((), (), s32[]{:S(2)}) async-start(), calls=%async_computation.18 | async-start | bytes 2654208 | tf_op jit(solution)/shard_map/reduce_scatter | solution.py:201
  976.7 319.7 %reduce-scatter.14.cloned.1.call-start = ((), (), s32[]{:S(2)}) async-start(), calls=%async_computation.21 | async-start | bytes 2654208 | tf_op jit(solution)/shard_map/reduce_scatter | solution.py:210
  981.3 497.9 %reduce-scatter.16.cloned.1.call-start = ((), (), s32[]{:S(2)}) async-start(), calls=%async_computation.22 | async-start | bytes 11943936 | tf_op jit(solution)/shard_map/reduce_scatter | solution.py:219
  991.2 670.6 %reduce-scatter.18.cloned.1.call-start = ((), (), s32[]{:S(2)}) async-start(), calls=%async_computation.23 | async-start | bytes 11943936 | tf_op jit(solution)/shard_map/reduce_scatter | solution.py:222
  1001.0 843.5 %reduce-scatter.20.cloned.1.call-start = ((), (), s32[]{:S(2)}) async-start(), calls=%async_computation.24 | async-start | bytes 11943936 | tf_op jit(solution)/shard_map/reduce_scatter | solution.py:225
  (55 other events, 680.6 us)
Sparse Core Ops, SparseCore 0:
  10.2 43.8 all-gather.9
  56.2 39.7 all-gather.11
  98.3 50.4 all-gather.7
  150.8 50.3 all-gather.13
  206.0 73.3 all-reduce.9
  281.4 152.2 all-gather.15
  435.8 150.2 all-gather.17
  588.4 150.2 all-gather.19
  749.5 72.9 all-reduce.11
  864.6 74.9 all-reduce.13
  969.4 46.1 all-reduce.15
  1018.9 64.8 reduce-scatter.9
  1087.2 63.8 reduce-scatter.11
  1155.0 68.6 reduce-scatter.7
  1227.6 68.7 reduce-scatter.13
  1299.9 179.2 reduce-scatter.15
  1482.6 179.1 reduce-scatter.17
  1665.3 179.1 reduce-scatter.19
where the time goes:
time: 1860 us; the launch traced here: 1850 us
  waiting for transfers between devices  1590 us (85%)
  matrix products  137 us (7%)
  other arithmetic  61 us (3%)
  blocking collectives  38.6 us (2%)
    reduce_scatter x1, waiting for transfers between devices, shards(): lax.psum_scatter(grad_w_gate.astype(jnp.bfloat16), 'dp', scatter_dimensio...  181 us
    reduce_scatter x1, waiting for transfers between devices, shards(): lax.psum_scatter(grad_w_down.astype(jnp.bfloat16), 'dp', scatter_dimensio...  180 us
    reduce_scatter x1, waiting for transfers between devices, shards(): lax.psum_scatter(grad_w_up.astype(jnp.bfloat16), 'dp', scatter_dimension=...  180 us
    all_gather x1, waiting for transfers between devices, shards(): lax.all_gather(w_gate, 'dp', axis=0, tiled=True)  146 us
    all_gather x1, waiting for transfers between devices, shards(): lax.all_gather(w_up, 'dp', axis=0, tiled=True)  142 us
    all_gather x1, waiting for transfers between devices, shards(): lax.all_gather(w_down, 'dp', axis=1, tiled=True)  140 us
    psum x1, waiting for transfers between devices, shards(): ffn_branch = lax.psum(matmul(hidden, down_full), 'tensor')  71.7 us
    psum x1, waiting for transfers between devices, shards(): attn_branch = lax.psum(matmul(mixed_flat, out_full), 'tensor')  71.2 us
  transfers between devices with their start and end apart: 18, of which 17 were waited for; matrix products, arithmetic and copies ran while one was open for 6% of the time, Pallas kernels for 0%

commit v1 on v0

--- a/solution.py
+++ b/solution.py
@@ -1,3 +1,4 @@
+import functools
 import math
 import jax
 import jax.numpy as jnp
@@ -11,6 +12,25 @@
 SOFT_CAP = 50.0
 QUERY_SCALE = 0.0625
 GELU_COEFF = 0.7978845608028654
+
+
+def answer_ends(work_x, which_axis):
+    sides = jax.lax.axis_size(which_axis)
+    bank = tuple(((k, (k + 1) % sides) for k in range(sides)))
+    v_next, outer = ([work_x], [work_x])
+    items = tuple(((k, (k - 1) % sides) for k in range(sides)))
+    for _ in range(sides // 2):
+        e_next = jax.lax.ppermute(v_next[-1], axis_name=which_axis, perm=bank)
+        v_next.append(e_next)
+    for _ in range((sides - 1) // 2):
+        f_next = jax.lax.ppermute(outer[-1], axis_name=which_axis, perm=items)
+        outer.append(f_next)
+    arr_out = jnp.concatenate([*v_next[::-1], *outer[1:]], axis=0)
+    top = jax.lax.axis_index(which_axis)
+    return jnp.roll(arr_out, shift=(top - sides // 2) * work_x.shape[0], axis=0)
+
+
+begin_the_boxes = functools.partial(answer_ends, which_axis="dp")
 
 
 def rms_scale(values, scales):
@@ -86,7 +106,7 @@
         lax.all_gather(w_value, "dp", axis=0, tiled=True),
         lax.all_gather(w_out, "dp", axis=1, tiled=True),
         lax.all_gather(w_gate, "dp", axis=0, tiled=True),
-        lax.all_gather(w_up, "dp", axis=0, tiled=True),
+        begin_the_boxes(w_up),
         lax.all_gather(w_down, "dp", axis=1, tiled=True),
     )
     query_full, key_full, value_full, out_full, gate_full, up_full, down_full = gathered

time: 1860 us -> 1790 us (0.962)
  waiting for transfers between devices: 1590 us -> 1470 us
  local copies, waits for them, and re-layouts: 13.6 us -> 44.8 us
    ppermute x0 -> x7, waiting for transfers between devices: none -> 230 us  [the longest x4 226 us: answer_ends(): e_next = jax.lax.ppermute(v_next[-1], axis_name=which_axis, perm=bank)]
    all_gather x1 -> x0, waiting for transfers between devices: 142 us -> none  [shards(): lax.all_gather(w_up, 'dp', axis=0, tiled=True)]
    all_gather x1, waiting for transfers between devices: 146 us -> 26 us  [shards(): lax.all_gather(w_gate, 'dp', axis=0, tiled=True)]
    psum x1, waiting for transfers between devices: 71.2 us -> 0.01 us  [shards(): attn_branch = lax.psum(matmul(mixed_flat, out_full), 'tensor')]
    unnamed x123 -> x148, local copies, waits for them, and re-layouts: 12.9 us -> 43 us
  transfers between devices with their start and end apart: 18 -> 24, of which waited for: 17 -> 20; matrix products, arithmetic and copies ran while one was open for 6% -> 8% of each run, Pallas kernels for 0% -> 0%
where the time goes in v1:
time: 1790 us; the launch traced here: 1780 us
  waiting for transfers between devices  1470 us (82%)
  matrix products  136 us (8%)
  other arithmetic  61 us (3%)
  local copies, waits for them, and re-layouts  44.8 us (3%)
  blocking collectives  38.6 us (2%)
    ppermute x4, waiting for transfers between devices, answer_ends(): e_next = jax.lax.ppermute(v_next[-1], axis_name=which_axis, perm=bank)  226 us
    reduce_scatter x1, waiting for transfers between devices, shards(): lax.psum_scatter(grad_w_gate.astype(jnp.bfloat16), 'dp', scatter_dimensio...  181 us
    reduce_scatter x1, waiting for transfers between devices, shards(): lax.psum_scatter(grad_w_up.astype(jnp.bfloat16), 'dp', scatter_dimension=...  180 us
    reduce_scatter x1, waiting for transfers between devices, shards(): lax.psum_scatter(grad_w_down.astype(jnp.bfloat16), 'dp', scatter_dimensio...  180 us
    all_gather x1, waiting for transfers between devices, shards(): lax.all_gather(w_down, 'dp', axis=1, tiled=True)  129 us
    psum x1, waiting for transfers between devices, shards(): ffn_branch = lax.psum(matmul(hidden, down_full), 'tensor')  71.5 us
    psum x1, waiting for transfers between devices, shards(): lax.psum(right_product(grad_gate, gate_back) + right_product(grad_up, up_...  71.3 us
    reduce_scatter x1, waiting for transfers between devices, shards(): lax.psum_scatter(grad_w_out.astype(jnp.bfloat16), 'dp', scatter_dimension...  71.1 us
  transfers between devices with their start and end apart: 24, of which 20 were waited for; matrix products, arithmetic and copies ran while one was open for 8% of the time, Pallas kernels for 0%

profile of v1, /device:TPU:0, one launch (start us, length us, event | category | flops | bytes accessed | tf_op | source)
XLA Modules:
  0.0 1782.9 jit_solution(4717562857470577595)
XLA Ops:
  15.7 38.3 %all-gather.9.cloned.1.call-done = bf16[2304,256]{1,0:T(8,128)(2,1)} async-done(((bf16[288,256]{1,0:T(8,128)(2,1)}), bf16[2304,256]{1,0:T(8,128)(2,1)}) %all-gather.9.cloned.1.call-update) | async-done | bytes 1179664 | tf_op jit(solution)/shard_map/all_gather | solution.py:105
  57.0 39.1 %all-gather.11.cloned.1.call-done = bf16[2304,256]{1,0:T(8,128)(2,1)} async-done(((bf16[288,256]{1,0:T(8,128)(2,1)}), bf16[2304,256]{1,0:T(8,128)(2,1)}) %all-gather.11.cloned.1.call-update) | async-done | bytes 1179664 | tf_op jit(solution)/shard_map/all_gather | solution.py:106
  98.0 50.8 %all-gather.7.cloned.1.call-done = bf16[2304,512]{1,0:T(8,128)(2,1)} async-done(((bf16[288,512]{1,0:T(8,128)(2,1)}), bf16[2304,512]{1,0:T(8,128)(2,1)}) %all-gather.7.cloned.1.call-update) | async-done | bytes 2359312 | tf_op jit(solution)/shard_map/all_gather | solution.py:104
  154.2 47.0 %all-gather.13.cloned.1.call-done = bf16[512,2304]{0,1:T(8,128)(2,1)} async-done(((bf16[512,288]{0,1:T(8,128)(2,1)}), bf16[512,2304]{0,1:T(8,128)(2,1)}) %all-gather.13.cloned.1.call-update) | async-done | bytes 2359312 | tf_op jit(solution)/shard_map/all_gather | solution.py:107
  207.8 31.5 %collective-permute-done = bf16[288,2304]{1,0:T(8,128)(2,1)S(1)} collective-permute-done((bf16[288,2304]{1,0:T(8,128)(2,1)S(1)}, bf16[288,2304]{1,0:T(8,128)(2,1)S(1)}, u32[]{:S(2)}, u32[]{:S(2)}) %collective-permute-start) | collective-permute-done | bytes 1327136 | tf_op jit(solution)/shard_map/ppermute | solution.py:23
  244.1 57.1 %collective-permute-done.1 = bf16[288,2304]{1,0:T(8,128)(2,1)S(1)} collective-permute-done((bf16[288,2304]{1,0:T(8,128)(2,1)S(1)}, bf16[288,2304]{1,0:T(8,128)(2,1)S(1)}, u32[]{:S(2)}, u32[]{:S(2)}) %collective-permute-start.1) | collective-permute-done | bytes 1327136 | tf_op jit(solution)/shard_map/ppermute | solution.py:23
  306.9 58.3 %collective-permute-done.2 = bf16[288,2304]{1,0:T(8,128)(2,1)} collective-permute-done((bf16[288,2304]{1,0:T(8,128)(2,1)S(1)}, bf16[288,2304]{1,0:T(8,128)(2,1)}, u32[]{:S(2)}, u32[]{:S(2)}) %collective-permute-start.2) | collective-permute-done | bytes 1327136 | tf_op jit(solution)/shard_map/ppermute | solution.py:23
  370.1 79.5 %collective-permute-done.3 = bf16[288,2304]{1,0:T(8,128)(2,1)} collective-permute-done((bf16[288,2304]{1,0:T(8,128)(2,1)}, bf16[288,2304]{1,0:T(8,128)(2,1)}, u32[]{:S(2)}, u32[]{:S(2)}) %collective-permute-start.3) | collective-permute-done | bytes 1327136 | tf_op jit(solution)/shard_map/ppermute | solution.py:23
  487.3 26.0 %all-gather.15.cloned.1.call-done = bf16[2304,2304]{1,0:T(8,128)(2,1)} async-done(((bf16[288,2304]{1,0:T(8,128)(2,1)}), bf16[2304,2304]{1,0:T(8,128)(2,1)}) %all-gather.15.cloned.1.call-update) | async-done | bytes 10616848 | tf_op jit(solution)/shard_map/all_gather | solution.py:108
  524.3 12.7 multiply_convert_fusion.1
  537.0 129.2 %all-gather.17.cloned.1.call-done = bf16[2304,2304]{0,1:T(8,128)(2,1)} async-done(((bf16[2304,288]{0,1:T(8,128)(2,1)}), bf16[2304,2304]{0,1:T(8,128)(2,1)}) %all-gather.17.cloned.1.call-update) | async-done | bytes 10616848 | tf_op jit(solution)/shard_map/all_gather | solution.py:110
  678.6 71.5 %all-reduce.12.cloned.1.call-done = f32[384,2304]{1,0:T(8,128)} async-done(((f32[384,2304]{1,0:T(8,128)}), f32[384,2304]{1,0:T(8,128)}) %all-reduce.12.cloned.1.call-update) | async-done | bytes 3538960 | tf_op jit(solution)/shard_map/psum | solution.py:148
  758.2 13.2 multiply_convert_fusion
  779.1 13.2 fusion.6
  796.1 71.3 %all-reduce.14.cloned.1.call-done = f32[384,2304]{1,0:T(8,128)} async-done(((f32[384,2304]{1,0:T(8,128)}), f32[384,2304]{1,0:T(8,128)}) %all-reduce.14.cloned.1.call-update) | async-done | bytes 3538960 | tf_op jit(solution)/shard_map/psum | solution.py:162
  931.2 10.7 convolution_convert_fusion
  947.9 38.6 %all-reduce.4 = (bf16[2304]{0:T(1024)(128)(2,1)}, bf16[2304]{0:T(1024)(128)(2,1)}, bf16[2304]{0:T(1024)(128)(2,1)}, bf16[2304]{0:T(1024)(128)(2,1)}) all-reduce(bf16[2304]{0:T(1024)(128)(2,1)} %get-tuple-element.19, bf16[2304]{0:T(1024)(128)(2,1)} %get-tuple-element.15, ...), channel_id=2, replica_groups=mesh['dp'=8,'tensor'=4] {'dp'}, use_global_device_ids=true, to_apply=%region_18.19.clone | all-reduce | flops 9216 | bytes 36864
  994.7 17.3 reduce-scatter.10.cloned.1.call-done
  1013.6 65.5 %reduce-scatter.12.cloned.1.call-done = bf16[288,256]{1,0:T(8,128)(2,1)} async-done(((bf16[2304,256]{1,0:T(8,128)(2,1)}), bf16[288,256]{1,0:T(8,128)(2,1)}) %reduce-scatter.12.cloned.1.call-update) | async-done | bytes 147472 | tf_op jit(solution)/shard_map/reduce_scatter | solution.py:227
  1080.8 71.1 %reduce-scatter.8.cloned.1.call-done = bf16[288,512]{1,0:T(8,128)(2,1)} async-done(((bf16[2304,512]{1,0:T(8,128)(2,1)}), bf16[288,512]{1,0:T(8,128)(2,1)}) %reduce-scatter.8.cloned.1.call-update) | async-done | bytes 294928 | tf_op jit(solution)/shard_map/reduce_scatter | solution.py:221
  1153.7 71.1 %reduce-scatter.14.cloned.1.call-done = bf16[512,288]{0,1:T(8,128)(2,1)} async-done(((bf16[512,2304]{0,1:T(8,128)(2,1)}), bf16[512,288]{0,1:T(8,128)(2,1)}) %reduce-scatter.14.cloned.1.call-update) | async-done | bytes 294928 | tf_op jit(solution)/shard_map/reduce_scatter | solution.py:230
  1226.7 180.9 %reduce-scatter.16.cloned.1.call-done = bf16[288,2304]{1,0:T(8,128)(2,1)} async-done(((bf16[2304,2304]{1,0:T(8,128)(2,1)}), bf16[288,2304]{1,0:T(8,128)(2,1)}) %reduce-scatter.16.cloned.1.call-update) | async-done | bytes 1327120 | tf_op jit(solution)/shard_map/reduce_scatter | solution.py:239
  1410.6 179.7 %reduce-scatter.18.cloned.1.call-done = bf16[288,2304]{1,0:T(8,128)(2,1)} async-done(((bf16[2304,2304]{1,0:T(8,128)(2,1)}), bf16[288,2304]{1,0:T(8,128)(2,1)}) %reduce-scatter.18.cloned.1.call-update) | async-done | bytes 1327120 | tf_op jit(solution)/shard_map/reduce_scatter | solution.py:242
  1593.3 179.6 %reduce-scatter.20.cloned.1.call-done = bf16[2304,288]{0,1:T(8,128)(2,1)} async-done(((bf16[2304,2304]{0,1:T(8,128)(2,1)}), bf16[2304,288]{0,1:T(8,128)(2,1)}) %reduce-scatter.20.cloned.1.call-update) | async-done | bytes 1327120 | tf_op jit(solution)/shard_map/reduce_scatter | solution.py:245
  (266 shorter events, 213.9 us)
Async XLA Ops:
  7.2 46.9 %all-gather.9.cloned.1.call-start = ((), (), s32[]{:S(2)}) async-start(), calls=%async_computation.8 | async-start | bytes 1327104 | tf_op jit(solution)/shard_map/all_gather | solution.py:105
  7.9 88.2 %all-gather.11.cloned.1.call-start = ((), (), s32[]{:S(2)}) async-start(), calls=%async_computation.9 | async-start | bytes 1327104 | tf_op jit(solution)/shard_map/all_gather | solution.py:106
  8.7 140.1 %all-gather.7.cloned.1.call-start = ((), (), s32[]{:S(2)}) async-start(), calls=%async_computation.7 | async-start | bytes 2654208 | tf_op jit(solution)/shard_map/all_gather | solution.py:104
  9.4 191.8 %all-gather.13.cloned.1.call-start = ((), (), s32[]{:S(2)}) async-start(), calls=%async_computation.10 | async-start | bytes 2654208 | tf_op jit(solution)/shard_map/all_gather | solution.py:107
  10.0 469.1 %all-reduce.10.cloned.1.call-start = ((), (), s32[]{:S(2)}) async-start(), calls=%async_computation.11 | async-start | bytes 7077888 | tf_op jit(solution)/shard_map/psum | solution.py:141
  205.8 307.4 %all-gather.15.cloned.1.call-start = ((), (), s32[]{:S(2)}) async-start(), calls=%async_computation.12 | async-start | bytes 11943936 | tf_op jit(solution)/shard_map/all_gather | solution.py:108
  206.4 459.8 %all-gather.17.cloned.1.call-start = ((), (), s32[]{:S(2)}) async-start(), calls=%async_computation.13 | async-start | bytes 11943936 | tf_op jit(solution)/shard_map/all_gather | solution.py:110
  207.2 542.9 %all-reduce.12.cloned.1.call-start = ((), (), s32[]{:S(2)}) async-start(), calls=%async_computation.14 | async-start | bytes 7077888 | tf_op jit(solution)/shard_map/psum | solution.py:148
  207.2 32.1 %collective-permute-start = (bf16[288,2304]{1,0:T(8,128)(2,1)S(1)}, bf16[288,2304]{1,0:T(8,128)(2,1)S(1)}, u32[]{:S(2)}, u32[]{:S(2)}) collective-permute-start(bf16[288,2304]{1,0:T(8,128)(2,1)S(1)} %copy-done.10), channel_id=1, source_target_pairs={{0,4},{4,8},{8,12},{12,16},{16,20},{20,24},{24,28},{28,0},{1,5},{5... | collective-permute-start | bytes 3981320 | tf_op jit(solution)/shard_map/ppermute | solution.py:23
  239.3 61.8 %collective-permute-start.1 = (bf16[288,2304]{1,0:T(8,128)(2,1)S(1)}, bf16[288,2304]{1,0:T(8,128)(2,1)S(1)}, u32[]{:S(2)}, u32[]{:S(2)}) collective-permute-start(bf16[288,2304]{1,0:T(8,128)(2,1)S(1)} %collective-permute-done), channel_id=1, source_target_pairs={{0,4},{4,8},{8,12},{12,16},{16,20},{20,24},{24,28},{28,0},{1,5},{5... | collective-permute-start | bytes 3981320 | tf_op jit(solution)/shard_map/ppermute | solution.py:23
  239.3 67.5 %collective-permute-start.4 = (bf16[288,2304]{1,0:T(8,128)(2,1)S(1)}, bf16[288,2304]{1,0:T(8,128)(2,1)}, u32[]{:S(2)}, u32[]{:S(2)}) collective-permute-start(bf16[288,2304]{1,0:T(8,128)(2,1)S(1)} %copy-done.10), channel_id=1, source_target_pairs={{0,28},{4,0},{8,4},{12,8},{16,12},{20,16},{24,20},{28,24},{1,29},{... | collective-permute-start | bytes 3981320 | tf_op jit(solution)/shard_map/ppermute | solution.py:26
  301.2 64.0 %collective-permute-start.2 = (bf16[288,2304]{1,0:T(8,128)(2,1)S(1)}, bf16[288,2304]{1,0:T(8,128)(2,1)}, u32[]{:S(2)}, u32[]{:S(2)}) collective-permute-start(bf16[288,2304]{1,0:T(8,128)(2,1)S(1)} %collective-permute-done.1), channel_id=1, source_target_pairs={{0,4},{4,8},{8,12},{12,16},{16,20},{20,24},{24,28},{28,0},{1,5},{5... | collective-permute-start | bytes 3981320 | tf_op jit(solution)/shard_map/ppermute | solution.py:23
  306.8 60.9 %collective-permute-start.5 = (bf16[288,2304]{1,0:T(8,128)(2,1)}, bf16[288,2304]{1,0:T(8,128)(2,1)}, u32[]{:S(2)}, u32[]{:S(2)}) collective-permute-start(bf16[288,2304]{1,0:T(8,128)(2,1)} %collective-permute-done.4), channel_id=1, source_target_pairs={{0,28},{4,0},{8,4},{12,8},{16,12},{20,16},{24,20},{28,24},{1,29},{... | collective-permute-start | bytes 3981320 | tf_op jit(solution)/shard_map/ppermute | solution.py:26
  365.2 84.4 %collective-permute-start.3 = (bf16[288,2304]{1,0:T(8,128)(2,1)}, bf16[288,2304]{1,0:T(8,128)(2,1)}, u32[]{:S(2)}, u32[]{:S(2)}) collective-permute-start(bf16[288,2304]{1,0:T(8,128)(2,1)} %collective-permute-done.2), channel_id=1, source_target_pairs={{0,4},{4,8},{8,12},{12,16},{16,20},{20,24},{24,28},{28,0},{1,5},{5... | collective-permute-start | bytes 3981320 | tf_op jit(solution)/shard_map/ppermute | solution.py:23
  367.8 95.5 %collective-permute-start.6 = (bf16[288,2304]{1,0:T(8,128)(2,1)}, bf16[288,2304]{1,0:T(8,128)(2,1)S(1)}, u32[]{:S(2)}, u32[]{:S(2)}) collective-permute-start(bf16[288,2304]{1,0:T(8,128)(2,1)} %collective-permute-done.5), channel_id=1, source_target_pairs={{0,28},{4,0},{8,4},{12,8},{16,12},{20,16},{24,20},{28,24},{1,29},{... | collective-permute-start | bytes 3981320 | tf_op jit(solution)/shard_map/ppermute | solution.py:26
  676.9 190.6 %all-reduce.14.cloned.1.call-start = ((), (), s32[]{:S(2)}) async-start(), calls=%async_computation.15 | async-start | bytes 7077888 | tf_op jit(solution)/shard_map/psum | solution.py:162
  792.4 151.5 %all-reduce.16.cloned.1.call-start = ((), (), s32[]{:S(2)}) async-start(), calls=%async_computation.16 | async-start | bytes 3538944 | tf_op jit(solution)/shard_map/psum | solution.py:213
  897.4 114.6 %reduce-scatter.10.cloned.1.call-start = ((), (), s32[]{:S(2)}) async-start(), calls=%async_computation.18 | async-start | bytes 1327104 | tf_op jit(solution)/shard_map/reduce_scatter | solution.py:224
  899.5 179.6 %reduce-scatter.12.cloned.1.call-start = ((), (), s32[]{:S(2)}) async-start(), calls=%async_computation.19 | async-start | bytes 1327104 | tf_op jit(solution)/shard_map/reduce_scatter | solution.py:227
  901.6 250.3 %reduce-scatter.8.cloned.1.call-start = ((), (), s32[]{:S(2)}) async-start(), calls=%async_computation.17 | async-start | bytes 2654208 | tf_op jit(solution)/shard_map/reduce_scatter | solution.py:221
  904.9 320.0 %reduce-scatter.14.cloned.1.call-start = ((), (), s32[]{:S(2)}) async-start(), calls=%async_computation.20 | async-start | bytes 2654208 | tf_op jit(solution)/shard_map/reduce_scatter | solution.py:230
  909.4 498.2 %reduce-scatter.16.cloned.1.call-start = ((), (), s32[]{:S(2)}) async-start(), calls=%async_computation.21 | async-start | bytes 11943936 | tf_op jit(solution)/shard_map/reduce_scatter | solution.py:239
  919.4 670.9 %reduce-scatter.18.cloned.1.call-start = ((), (), s32[]{:S(2)}) async-start(), calls=%async_computation.22 | async-start | bytes 11943936 | tf_op jit(solution)/shard_map/reduce_scatter | solution.py:242
  929.2 843.8 %reduce-scatter.20.cloned.1.call-start = ((), (), s32[]{:S(2)}) async-start(), calls=%async_computation.23 | async-start | bytes 11943936 | tf_op jit(solution)/shard_map/reduce_scatter | solution.py:245
  (66 other events, 1345.4 us)
Sparse Core Ops, SparseCore 0:
  10.2 43.8 all-gather.8
  56.2 39.7 all-gather.10
  98.3 50.4 all-gather.6
  150.8 50.3 all-gather.12
  206.0 73.3 all-reduce.9
  281.4 231.7 all-gather.14
  515.4 150.7 all-gather.16
  677.0 72.9 all-reduce.11
  792.5 74.9 all-reduce.13
  897.5 46.1 all-reduce.15
  947.1 64.7 reduce-scatter.9
  1015.2 63.8 reduce-scatter.11
  1083.2 68.6 reduce-scatter.7
  1155.8 68.9 reduce-scatter.13
  1228.3 179.2 reduce-scatter.15
  1411.1 179.1 reduce-scatter.17
  1593.7 179.1 reduce-scatter.19
